TPU v7x, 32 devices: a whole 2x2x4 slice. The times are simulated.
32 devices in a mesh: seq: 8 (over z, x), tp: 4 (over y, core).
Axes of the slice: x: 2, y: 2, z: 4, core: 2. Of those that a mesh axis runs over, the one named last changes fastest.
Arguments:
- queries: bfloat16 [1536, 4096], P('seq', 'tp'), may hold values from -80 to 80
- keys: bfloat16 [1536, 512], P('seq', 'tp'), may hold values from -4 to 4
- values: bfloat16 [1536, 512], P('seq', 'tp'), may hold values from -6 to 6
- segment_ids: int32 [1536], P('seq'), may hold values from 0 to 15, never falling along the last dimension, each value on 1 to 1152 neighbouring positions
- out_weight: bfloat16 [4096, 8192], P('tp', 'seq'), may hold values from -0.09375 to 0.09375
Outputs:
- projected: bfloat16 [1536, 8192], P('seq', 'tp')
Inputs may be any that keep to these rules, and one draw needn't show every extreme that they name: `segment_ids`: segment numbers never fall along the sequence and every number from 0 to 15 occurs; no document has more than 1152 tokens and one has exactly that many.
All inputs are finite; a program needn't handle non-finite values.
Results may differ from a plain program's by a relative error of at most 0.012.
Values may be sent and summed in bfloat16 or wider, within the bound.
A program may use at most 128 MiB of HBM per device.

v0:
```python
import functools
import math

import jax
import jax.numpy as jnp
import numpy as np
from jax import lax
from jax.experimental import pallas as pl
from jax.experimental.pallas import tpu as pltpu
from jax.sharding import PartitionSpec as P

HEADS = 32
KV_HEADS = 4
HEAD_DIM = 128
SEGMENTS = 16

rope_base = 500000.0
masked_score = -1e30
MESH = pl.DeviceIdType.MESH


def to_column(row_values, count):
    down = lax.broadcasted_iota(jnp.int32, (count, count), 0)
    across = lax.broadcasted_iota(jnp.int32, (count, count), 1)
    return jnp.sum(jnp.where(down == across, row_values, 0.0), axis=1, keepdims=True)


def doc_start_column(seg_all, block, members, rows):
    own = to_column(seg_all[block].astype(jnp.float32), rows)
    earlier = jnp.zeros((rows, rows), jnp.float32)
    for member in range(members):
        earlier = earlier + jnp.where(seg_all[member].astype(jnp.float32) < own, 1.0, 0.0)
    return jnp.sum(earlier, axis=1, keepdims=True)


def layer_kernel(
    members, slots, inverse_ref, q_ref, k_ref, v_ref, seg_ref, w_hbm, out_ref,
    seg_all, k_all, v_all, q_all, w_all, attended, top, total, acc,
    half_send, half_recv, half_own, piece, recv,
    seg_ss, seg_rs, k_ss, k_rs, v_ss, v_rs, q_ss, q_rs, w_ss, w_rs, own_sem,
    d_ss, d_rs, c_ss, c_rs,
):
    rows = q_ref.shape[0]
    heads = q_ref.shape[1] // HEAD_DIM
    width = w_hbm.shape[1]
    half = out_ref.shape[1] // 2
    tp_count = slots
    per = members // slots
    me = lax.axis_index("seq")
    g = lax.axis_index("tp")
    slot = lax.div(me, per)
    place = lax.rem(me, per)
    core = lax.rem(g, 2)
    sibling = g + 1 - 2 * core
    chunk_count = w_ss.shape[0] // max(per - 1, 1)
    chunk_rows = w_hbm.shape[0] // chunk_count

    barrier = pltpu.get_barrier_semaphore()
    for d in range(1, members):
        pl.semaphore_signal(
            barrier, inc=1, device_id={"seq": lax.rem(me + d, members)}, device_id_type=MESH
        )
    for e in range(1, tp_count):
        for d in range(slots):
            pl.semaphore_signal(
                barrier,
                inc=1,
                device_id={
                    "seq": lax.rem(slot + d, slots) * per + place,
                    "tp": lax.rem(g + e, tp_count),
                },
                device_id_type=MESH,
            )

    own_columns = pl.ds(pl.multiple_of(place * width, width), width)
    own_weight = pltpu.make_async_copy(w_hbm, w_all.at[:, own_columns], own_sem)
    own_weight.start()

    pl.semaphore_wait(barrier, members - 1 + (tp_count - 1) * slots)

    def to_member(source, target, send, recv_sem, d):
        return pltpu.make_async_remote_copy(
            src_ref=source,
            dst_ref=target,
            send_sem=send.at[d - 1],
            recv_sem=recv_sem.at[d - 1],
            device_id={"seq": lax.rem(me + d, members)},
            device_id_type=MESH,
        )

    my_tile = lax.div(me, 2)
    my_part = pl.ds(pl.multiple_of(lax.rem(me, 2) * rows, rows), rows)
    pending = []

    seg_copies = [to_member(seg_ref, seg_all.at[me], seg_ss, seg_rs, d) for d in range(1, members)]
    for copy in seg_copies:
        copy.start()
    v_copies = [
        to_member(v_ref, v_all.at[my_tile, my_part], v_ss, v_rs, d) for d in range(1, members)
    ]
    for copy in v_copies:
        copy.start()

    w_copies = []
    for c in range(chunk_count):
        band = pl.ds(c * chunk_rows, chunk_rows)
        for r in range(1, per):
            peer = slot * per + lax.rem(place + r, per)
            w_copies.append(
                pltpu.make_async_remote_copy(
                    src_ref=w_hbm.at[band],
                    dst_ref=w_all.at[band, own_columns],
                    send_sem=w_ss.at[c * (per - 1) + r - 1],
                    recv_sem=w_rs.at[c * (per - 1) + r - 1],
                    device_id={"seq": peer},
                    device_id_type=MESH,
                )
            )
    for copy in w_copies[: per - 1]:
        copy.start()

    seg_all[me] = seg_ref[...]
    v_all[my_tile, my_part] = v_ref[...]
    for copy in seg_copies:
        copy.wait_recv()

    row_index = lax.broadcasted_iota(jnp.int32, (rows, 1), 0)
    position = (me * rows + row_index).astype(jnp.float32) - doc_start_column(
        seg_all, me, members, rows
    )
    angle = position * inverse_ref[...]
    cosine = jnp.cos(angle)
    lane = lax.broadcasted_iota(jnp.int32, (rows, HEAD_DIM), 1)
    sine = jnp.where(lane < HEAD_DIM // 2, -1.0, 1.0) * jnp.sin(angle)

    def rotated(values):
        wide = values.astype(jnp.float32)
        return (wide * cosine + pltpu.roll(wide, HEAD_DIM // 2, 1) * sine).astype(jnp.bfloat16)

    k_all[my_tile, my_part] = rotated(k_ref[...])
    k_own = k_all.at[my_tile, my_part]
    k_copies = [to_member(k_own, k_own, k_ss, k_rs, d) for d in range(1, members)]
    for copy in k_copies:
        copy.start()
    for head in range(heads):
        lanes = slice(head * HEAD_DIM, (head + 1) * HEAD_DIM)
        q_all[slot, :, lanes] = rotated(q_ref[:, lanes])
    q_copies = []
    for d in range(1, slots):
        peer = lax.rem(slot + slots - d, slots) * per + place
        q_copies.append(
            pltpu.make_async_remote_copy(
                src_ref=q_all.at[slot],
                dst_ref=q_all.at[slot],
                send_sem=q_ss.at[d - 1],
                recv_sem=q_rs.at[d - 1],
                device_id={"seq": peer},
                device_id_type=MESH,
            )
        )
    for copy in q_copies:
        copy.start()
    for copy in w_copies[per - 1 :]:
        copy.start()

    for copy in v_copies:
        copy.wait_recv()
    for copy in k_copies:
        copy.wait_recv()

    tile_rows = k_all.shape[1]
    reach = -(-(3 * members * rows // 4 - 1) // rows)
    score_scale = math.log2(math.e) / math.sqrt(HEAD_DIM)

    def attend(block_slot):
        block = block_slot * per + place
        start = doc_start_column(seg_all, block, members, rows).astype(jnp.int32)
        query_index = block * rows + lax.broadcasted_iota(jnp.int32, (rows, tile_rows), 0)
        top[...] = jnp.full(top.shape, 0.5 * masked_score, jnp.float32)
        total[...] = jnp.zeros(total.shape, jnp.float32)
        acc[...] = jnp.zeros(acc.shape, jnp.float32)

        def tile(number, unused):
            key_index = number * tile_rows + lax.broadcasted_iota(
                jnp.int32, (rows, tile_rows), 1
            )
            visible = (key_index <= query_index) & (key_index >= start)
            bias = jnp.where(visible, 0.0, masked_score)
            key_tile = k_all[number]
            value_tile = v_all[number]
            for head in range(heads):
                lanes = slice(head * HEAD_DIM, (head + 1) * HEAD_DIM)
                scores = lax.dot_general(
                    q_all[block_slot, :, lanes],
                    key_tile,
                    (((1,), (1,)), ((), ())),
                    preferred_element_type=jnp.float32,
                )
                scores = scores * score_scale + bias
                old = top[head]
                new = jnp.maximum(old, jnp.max(scores, axis=1, keepdims=True))
                rescale = jnp.exp2(old - new)
                weights = jnp.exp2(
                    scores - jnp.concatenate([new] * (tile_rows // HEAD_DIM), axis=1)
                )
                added = weights[:, :HEAD_DIM]
                for part in range(1, tile_rows // HEAD_DIM):
                    added = added + weights[:, part * HEAD_DIM : (part + 1) * HEAD_DIM]
                top[head] = new
                total[head] = total[head] * rescale + added
                acc[head] = acc[head] * rescale + jnp.dot(
                    weights.astype(jnp.bfloat16), value_tile, preferred_element_type=jnp.float32
                )
            return unused

        first = lax.div(jnp.maximum(block - reach, 0), 2)
        lax.fori_loop(first, lax.div(block, 2) + 1, tile, 0)
        for head in range(heads):
            attended[block_slot, :, head * HEAD_DIM : (head + 1) * HEAD_DIM] = (
                acc[head] / jnp.sum(total[head], axis=1, keepdims=True)
            ).astype(jnp.bfloat16)

    for d in range(slots):
        if d > 0:
            q_copies[d - 1].wait_recv()
        attend(lax.rem(slot + d, slots))

    own_weight.wait()
    for copy in w_copies:
        copy.wait_recv()

    column_step = 256
    y_index = lax.div(g, 2)
    final_columns = pl.ds(pl.multiple_of(core * half, half), half)
    c_copies = []
    for d in list(range(1, slots)) + [0]:
        block_slot = lax.rem(slot + d, slots)
        block = block_slot * per + place
        for c in range(half // column_step):
            local_lanes = slice(c * column_step, (c + 1) * column_step)
            start = pl.multiple_of((1 - core) * half + c * column_step, column_step)
            half_send[d, :, local_lanes] = jnp.dot(
                attended[block_slot],
                w_all[:, pl.ds(start, column_step)],
                preferred_element_type=jnp.float32,
            ).astype(jnp.bfloat16)
        d2d = pltpu.make_async_remote_copy(
            src_ref=half_send.at[d],
            dst_ref=half_recv.at[d],
            send_sem=d_ss.at[d],
            recv_sem=d_rs.at[d],
            device_id={"tp": sibling},
            device_id_type=MESH,
        )
        d2d.start()
        pending.append(d2d)
        for c in range(half // column_step):
            local_lanes = slice(c * column_step, (c + 1) * column_step)
            start = pl.multiple_of(core * half + c * column_step, column_step)
            half_own[:, local_lanes] = jnp.dot(
                attended[block_slot],
                w_all[:, pl.ds(start, column_step)],
                preferred_element_type=jnp.float32,
            )
        d2d.wait_recv()
        piece[d] = (half_own[...] + half_recv[d].astype(jnp.float32)).astype(jnp.bfloat16)
        copy = pltpu.make_async_remote_copy(
            src_ref=piece.at[d],
            dst_ref=recv.at[y_index, :, final_columns],
            send_sem=c_ss.at[d],
            recv_sem=c_rs.at[g],
            device_id={"seq": block, "tp": slot},
            device_id_type=MESH,
        )
        if d > 0:
            copy.start()
        else:
            here = g == slot

            @pl.when(here)
            def _():
                recv[y_index, :, final_columns] = piece[0]

            @pl.when(jnp.logical_not(here))
            def _():
                copy.start()
        c_copies.append(copy)

    for source in range(tp_count):
        arrival = pltpu.make_async_remote_copy(
            src_ref=piece.at[0],
            dst_ref=recv.at[source // 2, :, (source % 2) * half : (source % 2 + 1) * half],
            send_sem=c_ss.at[0],
            recv_sem=c_rs.at[source],
            device_id={"seq": me, "tp": lax.rem(g + 1, tp_count)},
            device_id_type=MESH,
        )

        @pl.when(jnp.logical_or(g != source, g != slot))
        def _():
            arrival.wait_recv()

    result = recv[0].astype(jnp.float32)
    for part in range(1, tp_count // 2):
        result = result + recv[part].astype(jnp.float32)
    out_ref[...] = result.astype(out_ref.dtype)

    for copy in seg_copies + v_copies + k_copies + q_copies + w_copies + pending + c_copies[:-1]:
        copy.wait_send()

    @pl.when(g != slot)
    def _():
        c_copies[-1].wait_send()


def local(queries, keys, values, segment_ids, out_weight):
    rows = queries.shape[0]
    members = lax.axis_size("seq")
    slots = lax.axis_size("tp")
    per = members // slots
    heads = queries.shape[1] // HEAD_DIM
    out_width = out_weight.shape[1] * per
    half = out_width // 2
    chunk_count = 4
    exponent = np.arange(HEAD_DIM // 2, dtype=np.float32) * np.float32(2.0 / HEAD_DIM)
    inverse = np.power(np.float32(rope_base), -exponent).astype(np.float32)
    inverse = jnp.asarray(np.concatenate([inverse, inverse])[None, :])
    vmem = pl.BlockSpec(memory_space=pltpu.VMEM)
    bf16, f32 = jnp.bfloat16, jnp.float32
    dma = pltpu.SemaphoreType.DMA
    return pl.pallas_call(
        functools.partial(layer_kernel, members, slots),
        out_shape=jax.ShapeDtypeStruct((rows, out_width), bf16),
        in_specs=[vmem] * 5 + [pl.BlockSpec(memory_space=pl.ANY)],
        out_specs=vmem,
        scratch_shapes=[
            pltpu.VMEM((members, 1, rows), jnp.int32),
            pltpu.VMEM((members // 2, 2 * rows, HEAD_DIM), bf16),
            pltpu.VMEM((members // 2, 2 * rows, HEAD_DIM), bf16),
            pltpu.VMEM((slots, rows, queries.shape[1]), bf16),
            pltpu.VMEM((out_weight.shape[0], out_width), bf16),
            pltpu.VMEM((slots, rows, queries.shape[1]), bf16),
            pltpu.VMEM((heads, rows, HEAD_DIM), f32),
            pltpu.VMEM((heads, rows, HEAD_DIM), f32),
            pltpu.VMEM((heads, rows, HEAD_DIM), f32),
            pltpu.VMEM((slots, rows, half), bf16),
            pltpu.VMEM((slots, rows, half), bf16),
            pltpu.VMEM((rows, half), f32),
            pltpu.VMEM((slots, rows, half), bf16),
            pltpu.VMEM((slots // 2, rows, out_width), bf16),
        ]
        + [dma((members - 1,))] * 6
        + [dma((slots - 1,))] * 2
        + [dma((chunk_count * (per - 1),))] * 2
        + [dma(())]
        + [dma((slots,))] * 4,
        compiler_params=pltpu.CompilerParams(
            collective_id=0, has_side_effects=True, vmem_limit_bytes=60 * 1024 * 1024
        ),
    )(inverse, queries, keys, values, segment_ids.reshape(1, rows), out_weight)


def solution(mesh):
    return jax.shard_map(
        local,
        mesh=mesh,
        in_specs=(P("seq", "tp"), P("seq", "tp"), P("seq", "tp"), P("seq"), P("tp", "seq")),
        out_specs=P("seq", "tp"),
        check_vma=False,
    )
```

profile of v0, /device:TPU:25, one launch (start us, length us, event | category | flops | bytes accessed | tf_op | source)
XLA Modules:
  0.0 111.5 jit_solution(15511910514908570012)
XLA Ops:
  0.0 109.4 %shard_map.64 = bf16[192,2048]{1,0:T(8,128)(2,1)} custom-call(f32[1,128]{1,0:T(1,128)} %constant.2.clone.inverse_ref, bf16[192,1024]{1,0:T(8,128)(2,1)} %q_ref.1, bf16[192,128]{1,0:T(8,128)(2,1)} %k_ref.1, bf16[192,128]{1,0:T(8,128)(2,1)} %v_ref.1, s32[1,192]{1,0:T(1,128)} %bitcast.1, bf16[1024,1024]{1,0:T(8,128)(2,1)} %w_hbm.1), custom_call_target="tpu_custom_call" | custom-call | tf_op jit(solution)/shard_map/pallas_call | solution.py:331
  109.4 2.1 %copy.8 = bf16[192,2048]{1,0:T(8,128)(2,1)} copy(bf16[192,2048]{1,0:T(8,128)(2,1)} %shard_map.64) | data formatting | bytes 1572864
where the time goes:
time: 112 us; the launch traced here: 111 us
  Pallas kernels  109 us (97%)
  local copies, waits for them, and re-layouts  2.09 us (2%)
    pallas_call x1, Pallas kernels, local(): pl.pallas_call(functools.partial(layer_kernel, members, slots), out_shape...  109 us

commit v1 on v0

v1 whole, which is shorter than its diff:
```python
import functools
import math

import jax
import jax.numpy as jnp
import numpy as np
from jax import lax
from jax.experimental import pallas as pl
from jax.experimental.pallas import tpu as pltpu
from jax.sharding import PartitionSpec as P

HEADS = 32
KV_HEADS = 4
HEAD_DIM = 128
SEGMENTS = 16

rope_base = 500000.0
masked_score = -1e30
MESH = pl.DeviceIdType.MESH


def to_column(row_values, count):
    down = lax.broadcasted_iota(jnp.int32, (count, count), 0)
    across = lax.broadcasted_iota(jnp.int32, (count, count), 1)
    return jnp.sum(jnp.where(down == across, row_values, 0.0), axis=1, keepdims=True)


def doc_start_column(seg_all, block, members, rows):
    own = to_column(seg_all[block].astype(jnp.float32), rows)
    earlier = jnp.zeros((rows, rows), jnp.float32)
    for member in range(members):
        earlier = earlier + jnp.where(seg_all[member].astype(jnp.float32) < own, 1.0, 0.0)
    return jnp.sum(earlier, axis=1, keepdims=True)


def layer_kernel(
    members, slots, inverse_hbm, q_hbm, k_hbm, v_hbm, seg_hbm, w_hbm, recv,
    inverse_ref, q_ref, k_ref, seg_all, k_all, v_all, q_all, w_all, attended,
    top, total, acc, scores_ref, half_send, half_recv, half_own, piece, in_sems,
    seg_ss, seg_rs, k_ss, k_rs, v_ss, v_rs, k2_ss, k2_rs, v2_ss, v2_rs, q_ss, q_rs,
    w_ss, w_rs, own_sem, d_ss, d_rs, c_ss, c_rs,
):
    rows = q_ref.shape[0]
    heads = q_ref.shape[1] // HEAD_DIM
    width = w_hbm.shape[1]
    out_width = recv.shape[2]
    tp_count = slots
    per = members // slots
    me = lax.axis_index("seq")
    g = lax.axis_index("tp")
    slot = lax.div(me, per)
    place = lax.rem(me, per)
    core = lax.rem(g, 2)
    sibling = g + 1 - 2 * core
    chunk_count = w_ss.shape[0] // (per - 1)

    def part_of(ref, block):
        return ref.at[
            lax.div(block, 2), pl.ds(pl.multiple_of(lax.rem(block, 2) * rows, rows), rows)
        ]

    inputs = [
        (seg_hbm, seg_all.at[me]),
        (v_hbm, part_of(v_all, me)),
        (k_hbm, k_ref),
        (inverse_hbm, inverse_ref),
        (q_hbm, q_ref),
    ]
    inputs = [
        pltpu.make_async_copy(source, target, in_sems.at[i])
        for i, (source, target) in enumerate(inputs)
    ]
    for copy in inputs:
        copy.start()

    barrier = pltpu.get_barrier_semaphore()
    for d in range(1, members):
        pl.semaphore_signal(
            barrier, inc=1, device_id={"seq": lax.rem(me + d, members)}, device_id_type=MESH
        )
    for e in range(1, tp_count):
        for d in range(slots):
            pl.semaphore_signal(
                barrier,
                inc=1,
                device_id={
                    "seq": lax.rem(slot + d, slots) * per + place,
                    "tp": lax.rem(g + e, tp_count),
                },
                device_id_type=MESH,
            )

    own_columns = pl.ds(pl.multiple_of(place * width, width), width)
    own_weight = pltpu.make_async_copy(w_hbm, w_all.at[:, own_columns], own_sem)
    own_weight.start()
    for copy in inputs:
        copy.wait()

    with jax.named_scope("barrier_wait"):
        pl.semaphore_wait(barrier, members - 1 + (tp_count - 1) * slots)

    def send(source, target, send_sem, recv_sem, peer):
        return pltpu.make_async_remote_copy(
            src_ref=source,
            dst_ref=target,
            send_sem=send_sem,
            recv_sem=recv_sem,
            device_id={"seq": peer},
            device_id_type=MESH,
        )

    def from_slot(d):
        return lax.rem(slot + slots - d, slots) * per + place

    def to_slots(source, target, ss, rs):
        return [
            send(source, target, ss.at[d - 1], rs.at[d - 1], lax.rem(slot + d, slots) * per + place)
            for d in range(1, slots)
        ]

    def relay(ref, d, ss, rs):
        block = from_slot(d)
        return [
            send(
                part_of(ref, block),
                part_of(ref, block),
                ss.at[d * (per - 1) + r - 1],
                rs.at[d * (per - 1) + r - 1],
                slot * per + lax.rem(place + r, per),
            )
            for r in range(1, per)
        ]

    def start_all(copies):
        for copy in copies:
            copy.start()
        return copies

    started = []
    seg_copies = start_all(
        [
            send(seg_all.at[me], seg_all.at[me], seg_ss.at[d - 1], seg_rs.at[d - 1], lax.rem(me + d, members))
            for d in range(1, members)
        ]
    )
    started += seg_copies
    v_own = part_of(v_all, me)
    v_copies = start_all(to_slots(v_own, v_own, v_ss, v_rs))
    started += v_copies
    v_relays = start_all(relay(v_all, 0, v2_ss, v2_rs))

    units = c_rs.shape[1]
    if units > 1:
        unit_width = out_width // units
        own_units = units // per
        unit_starts = [
            lax.rem(place + u // own_units, per) * width + (u % own_units) * unit_width
            for u in range(units)
        ]
    else:
        unit_width, own_units, unit_starts = width, 1, [0]
    half = piece.shape[2]
    column_chunks = width // unit_width
    bands = chunk_count // column_chunks
    band_rows = w_hbm.shape[0] // bands
    w_copies = []
    for c in range(chunk_count):
        band = pl.ds((c % bands) * band_rows, band_rows)
        first = (c // bands) * unit_width
        target_columns = pl.ds(pl.multiple_of(place * width + first, unit_width), unit_width)
        for r in range(1, per):
            w_copies.append(
                send(
                    w_hbm.at[band, first : first + unit_width],
                    w_all.at[band, target_columns],
                    w_ss.at[c * (per - 1) + r - 1],
                    w_rs.at[c * (per - 1) + r - 1],
                    slot * per + lax.rem(place + r, per),
                )
            )
    early = 2 * (per - 1)
    start_all(w_copies[:early])

    with jax.named_scope("seg_wait"):
        for copy in seg_copies:
            copy.wait_recv()

    row_index = lax.broadcasted_iota(jnp.int32, (rows, 1), 0)
    position = (me * rows + row_index).astype(jnp.float32) - doc_start_column(
        seg_all, me, members, rows
    )
    angle = position * inverse_ref[...]
    cosine = jnp.cos(angle)
    lane = lax.broadcasted_iota(jnp.int32, (rows, HEAD_DIM), 1)
    sine = jnp.where(lane < HEAD_DIM // 2, -1.0, 1.0) * jnp.sin(angle)

    def rotated(values):
        wide = values.astype(jnp.float32)
        return (wide * cosine + pltpu.roll(wide, HEAD_DIM // 2, 1) * sine).astype(jnp.bfloat16)

    k_own = part_of(k_all, me)
    k_own[...] = rotated(k_ref[...])
    k_copies = start_all(to_slots(k_own, k_own, k_ss, k_rs))
    started += k_copies
    k_relays = start_all(relay(k_all, 0, k2_ss, k2_rs))

    for head in range(heads):
        lanes = slice(head * HEAD_DIM, (head + 1) * HEAD_DIM)
        q_all[slot, :, lanes] = rotated(q_ref[:, lanes])
    pair = slot + 1 - 2 * lax.rem(slot, 2)
    inner = lax.rem(lax.div(slot + 1, 2), 2)
    third = 2 - lax.div(slot, 2)
    fourth = (slots - 1) * (1 - lax.div(slot, 2))

    def send_queries(block_slot, target_slot, index):
        return send(
            q_all.at[block_slot],
            q_all.at[block_slot],
            q_ss.at[index],
            q_rs.at[block_slot],
            target_slot * per + place,
        )

    first_queries, second_queries = send_queries(slot, pair, 0), send_queries(slot, third, 1)
    first_queries.start()
    started.append(second_queries)

    @pl.when(inner == 1)
    def _():
        second_queries.start()


    for d in range(1, slots):
        with jax.named_scope(f"v_wait{d}"):
            v_copies[d - 1].wait_recv()
        v_relays += start_all(relay(v_all, d, v2_ss, v2_rs))
    for d in range(1, slots):
        with jax.named_scope(f"k_wait{d}"):
            k_copies[d - 1].wait_recv()
        k_relays += start_all(relay(k_all, d, k2_ss, k2_rs))
    started += v_relays + k_relays
    start_all(w_copies[early:])
    with jax.named_scope("kv_relay_wait"):
        for copy in v_relays + k_relays:
            copy.wait_recv()

    tile_rows = k_all.shape[1]
    reach = -(-(3 * members * rows // 4 - 1) // rows)
    score_scale = math.log2(math.e) / math.sqrt(HEAD_DIM)

    group = scores_ref.shape[1]

    def attend(block_slot):
        block = block_slot * per + place
        start = doc_start_column(seg_all, block, members, rows).astype(jnp.int32)
        query_index = block * rows + lax.broadcasted_iota(jnp.int32, (rows, tile_rows), 0)
        first = lax.div(jnp.maximum(block - reach, 0), 2)
        last = lax.div(block, 2) + 1
        parts = [slice(p * HEAD_DIM, (p + 1) * HEAD_DIM) for p in range(tile_rows // HEAD_DIM)]
        for base in range(0, heads, group):
            top[...] = jnp.full(top.shape, masked_score, jnp.float32)
            total[...] = jnp.zeros(total.shape, jnp.float32)
            acc[...] = jnp.zeros(acc.shape, jnp.float32)

            def score_tile(number, unused):
                key_index = number * tile_rows + lax.broadcasted_iota(
                    jnp.int32, (rows, tile_rows), 1
                )
                visible = (key_index <= query_index) & (key_index >= start)
                bias = jnp.where(visible, 0.0, masked_score)
                key_tile = k_all[number]
                for head in range(group):
                    lanes = slice((base + head) * HEAD_DIM, (base + head + 1) * HEAD_DIM)
                    scores = lax.dot_general(
                        q_all[block_slot, :, lanes],
                        key_tile,
                        (((1,), (1,)), ((), ())),
                        preferred_element_type=jnp.float32,
                    )
                    scores = scores * score_scale + bias
                    scores_ref[number, head] = scores
                    best = top[head]
                    for part in parts:
                        best = jnp.maximum(best, scores[:, part])
                    top[head] = best
                return unused

            lax.fori_loop(first, last, score_tile, 0)
            for head in range(group):
                top[head] = jnp.broadcast_to(
                    jnp.max(top[head], axis=1, keepdims=True), (rows, HEAD_DIM)
                )

            def value_tile(number, unused):
                values = v_all[number]
                for head in range(group):
                    weights = jnp.exp2(
                        scores_ref[number, head] - jnp.concatenate([top[head]] * len(parts), axis=1)
                    )
                    added = total[head]
                    for part in parts:
                        added = added + weights[:, part]
                    total[head] = added
                    acc[head] = acc[head] + jnp.dot(
                        weights.astype(jnp.bfloat16), values, preferred_element_type=jnp.float32
                    )
                return unused

            lax.fori_loop(first, last, value_tile, 0)
            for head in range(group):
                lanes = slice((base + head) * HEAD_DIM, (base + head + 1) * HEAD_DIM)
                attended[block_slot, :, lanes] = (
                    acc[head] / jnp.sum(total[head], axis=1, keepdims=True)
                ).astype(jnp.bfloat16)

    y_index = lax.div(g, 2)
    step = min(256, half)
    pair_copies, c_copies = [], []
    held = []

    def multiply(block_slot, unit, order):
        index = order * units + unit
        buffer = len(pair_copies) % half_own.shape[0]
        kept = unit_starts[unit] + core * half
        given = unit_starts[unit] + (1 - core) * half
        for c in range(half // step):
            half_send[index, :, c * step : (c + 1) * step] = jnp.dot(
                attended[block_slot],
                w_all[:, pl.ds(pl.multiple_of(given + c * step, step), step)],
                preferred_element_type=jnp.float32,
            ).astype(jnp.bfloat16)
        across = pltpu.make_async_remote_copy(
            src_ref=half_send.at[index],
            dst_ref=half_recv.at[index],
            send_sem=d_ss.at[index],
            recv_sem=d_rs.at[index],
            device_id={"tp": sibling},
            device_id_type=MESH,
        )
        across.start()
        pair_copies.append(across)
        for c in range(half // step):
            half_own[buffer, :, c * step : (c + 1) * step] = jnp.dot(
                attended[block_slot],
                w_all[:, pl.ds(pl.multiple_of(kept + c * step, step), step)],
                preferred_element_type=jnp.float32,
            )
        held.append((block_slot, unit, order, index, buffer, kept, across))

    def finish():
        block_slot, unit, order, index, buffer, kept, across = held.pop(0)
        with jax.named_scope(f"across_wait{index}"):
            across.wait_recv()
        piece[index] = (half_own[buffer] + half_recv[index].astype(jnp.float32)).astype(
            jnp.bfloat16
        )
        target = recv.at[y_index, :, pl.ds(pl.multiple_of(kept, half), half)]
        copy = pltpu.make_async_remote_copy(
            src_ref=piece.at[index],
            dst_ref=target,
            send_sem=c_ss.at[index],
            recv_sem=c_rs.at[g, unit],
            device_id={"seq": block_slot * per + place, "tp": slot},
            device_id_type=MESH,
        )
        if order == 0:

            @pl.when(g == slot)
            def _():
                target[...] = piece[index]

            @pl.when(g != slot)
            def _():
                copy.start()
        else:
            copy.start()
        c_copies.append((order, copy))

    def pass_on(block_slot, index):
        copy = send_queries(block_slot, pair, index)

        @pl.when(inner == 1)
        def _():
            with jax.named_scope(f"forward_wait{index}"):
                copy.wait_recv()
            copy.start()

        return copy

    slot_order = [slot, pair, third, fourth]
    query_forwards = []
    for order, block_slot in enumerate(slot_order):
        if order > 0:
            arrived = send_queries(block_slot, pair, 0)
            if order == 1:
                with jax.named_scope(f"q_wait{order}"):
                    arrived.wait_recv()
            else:

                @pl.when(inner == 0)
                def _():
                    with jax.named_scope(f"q_wait{order}"):
                        arrived.wait_recv()
        with jax.named_scope(f"attend{order}"):
            attend(block_slot)
        if order == 0:
            own_weight.wait()
        if units > 1:
            with jax.named_scope(f"product{order}"):
                for unit in range(own_units):
                    multiply(block_slot, unit, order)
                    if len(held) > 1:
                        finish()
                while held:
                    finish()
        if order == 0:
            first_queries.wait_send()

            @pl.when(inner == 0)
            def _():
                second_queries.start()

            query_forwards.append(pass_on(third, 2))
        if order == 1:
            query_forwards.append(pass_on(fourth, 3))

    late = own_units if units > 1 else 0
    for unit in range(late, units):
        chunk = (unit % own_units) * bands
        sender = unit // own_units - 1
        with jax.named_scope(f"w_wait{unit}"):
            for c in range(chunk_count):
                for r in range(per - 1):
                    if units == 1 or (chunk <= c < chunk + bands and r == per - 2 - sender):
                        w_copies[c * (per - 1) + r].wait_recv()
        for order in list(range(1, slots)) + [0]:
            multiply(slot_order[order], unit, order)
            if len(held) > 1:
                finish()
    while held:
        finish()

    for source in range(tp_count):
        for unit in range(units):
            arrival = pltpu.make_async_remote_copy(
                src_ref=piece.at[0],
                dst_ref=recv.at[source // 2, :, :half],
                send_sem=c_ss.at[0],
                recv_sem=c_rs.at[source, unit],
                device_id={"seq": me, "tp": sibling},
                device_id_type=MESH,
            )

            @pl.when(jnp.logical_or(g != source, g != slot))
            def _():
                with jax.named_scope(f"arrive{source}_{unit}"):
                    arrival.wait_recv()

    with jax.named_scope("send_waits"):
        for copy in started + w_copies + pair_copies:
            copy.wait_send()
        for order, copy in c_copies:
            if order > 0:
                copy.wait_send()

        @pl.when(g != slot)
        def _():
            for order, copy in c_copies:
                if order == 0:
                    copy.wait_send()

        @pl.when(inner == 1)
        def _():
            for copy in query_forwards:
                copy.wait_send()


def add_kernel(pieces, out_ref):
    result = pieces[0].astype(jnp.float32)
    for part in range(1, pieces.shape[0]):
        result = result + pieces[part].astype(jnp.float32)
    out_ref[...] = result.astype(out_ref.dtype)


def local(queries, keys, values, segment_ids, out_weight):
    rows = queries.shape[0]
    members = lax.axis_size("seq")
    slots = lax.axis_size("tp")
    per = members // slots
    heads = queries.shape[1] // HEAD_DIM
    out_width = out_weight.shape[1] * per
    units = out_width // 512 if out_weight.shape[1] % 512 == 0 else 1
    half = out_width // units // 2
    chunk_count = 16
    tiles = members // 2
    group = heads
    while group > 1 and tiles * group * rows * 2 * rows * 4 > 20 * 1024 * 1024:
        group //= 2
    exponent = np.arange(HEAD_DIM // 2, dtype=np.float32) * np.float32(2.0 / HEAD_DIM)
    inverse = np.power(np.float32(rope_base), -exponent).astype(np.float32)
    inverse = jnp.asarray(np.concatenate([inverse, inverse])[None, :])
    vmem = pl.BlockSpec(memory_space=pltpu.VMEM)
    bf16, f32 = jnp.bfloat16, jnp.float32
    dma = pltpu.SemaphoreType.DMA
    pieces = pl.pallas_call(
        functools.partial(layer_kernel, members, slots),
        out_shape=jax.ShapeDtypeStruct((slots // 2, rows, out_width), bf16),
        in_specs=[pl.BlockSpec(memory_space=pl.ANY)] * 6,
        out_specs=vmem,
        scratch_shapes=[
            pltpu.VMEM((1, HEAD_DIM), f32),
            pltpu.VMEM(queries.shape, bf16),
            pltpu.VMEM(keys.shape, bf16),
            pltpu.VMEM((members, 1, rows), jnp.int32),
            pltpu.VMEM((tiles, 2 * rows, HEAD_DIM), bf16),
            pltpu.VMEM((tiles, 2 * rows, HEAD_DIM), bf16),
            pltpu.VMEM((slots, rows, queries.shape[1]), bf16),
            pltpu.VMEM((out_weight.shape[0], out_width), bf16),
            pltpu.VMEM((slots, rows, queries.shape[1]), bf16),
            pltpu.VMEM((group, rows, HEAD_DIM), f32),
            pltpu.VMEM((group, rows, HEAD_DIM), f32),
            pltpu.VMEM((group, rows, HEAD_DIM), f32),
            pltpu.VMEM((tiles, group, rows, 2 * rows), f32),
            pltpu.VMEM((slots * units, rows, half), bf16),
            pltpu.VMEM((slots * units, rows, half), bf16),
            pltpu.VMEM((2, rows, half), f32),
            pltpu.VMEM((slots * units, rows, half), bf16),
            dma((5,)),
        ]
        + [dma((members - 1,))] * 2
        + [dma((slots - 1,))] * 4
        + [dma((slots * (per - 1),))] * 4
        + [dma((slots,))] * 2
        + [dma((chunk_count * (per - 1),))] * 2
        + [dma(())]
        + [dma((slots * units,))] * 3
        + [dma((slots, units))],
        compiler_params=pltpu.CompilerParams(
            collective_id=0, has_side_effects=True, vmem_limit_bytes=60 * 1024 * 1024
        ),
    )(inverse, queries, keys, values, segment_ids.reshape(1, rows), out_weight)
    band = rows // 4
    return pl.pallas_call(
        add_kernel,
        grid=(rows // band,),
        out_shape=jax.ShapeDtypeStruct((rows, out_width), bf16),
        in_specs=[pl.BlockSpec((slots // 2, band, out_width), lambda i: (0, i, 0))],
        out_specs=pl.BlockSpec((band, out_width), lambda i: (i, 0)),
    )(pieces)


def solution(mesh):
    return jax.shard_map(
        local,
        mesh=mesh,
        in_specs=(P("seq", "tp"), P("seq", "tp"), P("seq", "tp"), P("seq"), P("tp", "seq")),
        out_specs=P("seq", "tp"),
        check_vma=False,
    )
```

time: 112 us -> 84.6 us (0.76)
  the two profiles are of different devices: /device:TPU:25 before, /device:TPU:4 now
where the time goes in v1:
time: 84.6 us; the launch traced here: 83.2 us
  Pallas kernels  83.2 us (98%)
    pallas_call x1, Pallas kernels, local(): pl.pallas_call(functools.partial(layer_kernel, members, slots), out_shape...  79.7 us
    pallas_call x1, Pallas kernels, local(): pl.pallas_call(add_kernel, grid=(rows // band,), out_shape=jax.ShapeDtype...  3.48 us

profile of v1, /device:TPU:4, one launch (start us, length us, event | category | flops | bytes accessed | tf_op | source)
XLA Modules:
  0.0 83.2 jit_solution(15973191006398823874)
XLA Ops:
  0.0 79.7 %shard_map.64.pieces = bf16[2,192,2048]{2,1,0:T(8,128)(2,1)} custom-call(f32[1,128]{1,0:T(1,128)} %constant.2.clone.inverse_hbm, bf16[192,1024]{1,0:T(8,128)(2,1)} %q_hbm.1, bf16[192,128]{1,0:T(8,128)(2,1)} %k_hbm.1, bf16[192,128]{1,0:T(8,128)(2,1)} %v_hbm.1, s32[1,192]{1,0:T(1,128)} %bitcast.1, bf16[1024,1024]{1,0:T(8,128)(2,1)} %w_hbm.1), custom_call_target="tpu_custom_call" | custom-call | tf_op jit(solution)/shard_map/pallas_call | solution.py:505
  79.7 3.5 %shard_map.65 = bf16[192,2048]{1,0:T(8,128)(2,1)} custom-call(bf16[2,192,2048]{2,1,0:T(8,128)(2,1)} %shard_map.64.pieces), custom_call_target="tpu_custom_call" | custom-call | tf_op jit(solution)/shard_map/pallas_call | solution.py:543

commit v2 on v1

--- a/solution.py
+++ b/solution.py
@@ -38,7 +38,7 @@
     inverse_ref, q_ref, k_ref, seg_all, k_all, v_all, q_all, w_all, attended,
     top, total, acc, scores_ref, half_send, half_recv, half_own, piece, in_sems,
     seg_ss, seg_rs, k_ss, k_rs, v_ss, v_rs, k2_ss, k2_rs, v2_ss, v2_rs, q_ss, q_rs,
-    w_ss, w_rs, own_sem, d_ss, d_rs, c_ss, c_rs,
+    w_ss, w_rs, own_sem, clear, d_ss, d_rs, c_ss, c_rs,
 ):
     rows = q_ref.shape[0]
     heads = q_ref.shape[1] // HEAD_DIM
@@ -178,7 +178,7 @@
                     slot * per + lax.rem(place + r, per),
                 )
             )
-    early = 2 * (per - 1)
+    early = per - 1
     start_all(w_copies[:early])
 
     with jax.named_scope("seg_wait"):
@@ -223,7 +223,7 @@
 
     first_queries, second_queries = send_queries(slot, pair, 0), send_queries(slot, third, 1)
     first_queries.start()
-    started.append(second_queries)
+    started.append(first_queries)
 
     @pl.when(inner == 1)
     def _():
@@ -387,24 +387,7 @@
 
         return copy
 
-    slot_order = [slot, pair, third, fourth]
-    query_forwards = []
-    for order, block_slot in enumerate(slot_order):
-        if order > 0:
-            arrived = send_queries(block_slot, pair, 0)
-            if order == 1:
-                with jax.named_scope(f"q_wait{order}"):
-                    arrived.wait_recv()
-            else:
-
-                @pl.when(inner == 0)
-                def _():
-                    with jax.named_scope(f"q_wait{order}"):
-                        arrived.wait_recv()
-        with jax.named_scope(f"attend{order}"):
-            attend(block_slot)
-        if order == 0:
-            own_weight.wait()
+    def own_products(block_slot, order):
         if units > 1:
             with jax.named_scope(f"product{order}"):
                 for unit in range(own_units):
@@ -413,16 +396,57 @@
                         finish()
                 while held:
                     finish()
-        if order == 0:
-            first_queries.wait_send()
+
+    second_block = pair + inner * (third - pair)
+    third_block = third + inner * (fourth - third)
+    fourth_block = fourth + inner * (pair - fourth)
+    query_forwards = []
+
+    def wait_queries(block_slot, only_outer=False):
+        arrived = send_queries(block_slot, pair, 0)
+        if only_outer:
 
             @pl.when(inner == 0)
             def _():
-                second_queries.start()
-
-            query_forwards.append(pass_on(third, 2))
-        if order == 1:
-            query_forwards.append(pass_on(fourth, 3))
+                with jax.named_scope("q_wait_outer"):
+                    arrived.wait_recv()
+        else:
+            with jax.named_scope("q_wait_last"):
+                arrived.wait_recv()
+
+    with jax.named_scope("attend0"):
+        attend(slot)
+
+    @pl.when(inner == 1)
+    def _():
+        with jax.named_scope("second_q_sent"):
+            second_queries.wait_send()
+        pl.semaphore_signal(
+            clear, inc=1, device_id={"seq": pair * per + place}, device_id_type=MESH
+        )
+
+    @pl.when(inner == 0)
+    def _():
+        with jax.named_scope("clear_wait"):
+            pl.semaphore_wait(clear, 1)
+        second_queries.start()
+
+    query_forwards.append(pass_on(third, 2))
+    wait_queries(pair, only_outer=True)
+    with jax.named_scope("attend1"):
+        attend(second_block)
+    own_weight.wait()
+    own_products(second_block, 1)
+    own_products(slot, 0)
+    query_forwards.append(pass_on(fourth, 3))
+    wait_queries(third, only_outer=True)
+    with jax.named_scope("attend2"):
+        attend(third_block)
+    own_products(third_block, 2)
+    wait_queries(fourth_block)
+    with jax.named_scope("attend3"):
+        attend(fourth_block)
+    own_products(fourth_block, 3)
 
     late = own_units if units > 1 else 0
     for unit in range(late, units):
@@ -433,8 +457,8 @@
                 for r in range(per - 1):
                     if units == 1 or (chunk <= c < chunk + bands and r == per - 2 - sender):
                         w_copies[c * (per - 1) + r].wait_recv()
-        for order in list(range(1, slots)) + [0]:
-            multiply(slot_order[order], unit, order)
+        for order, block_slot in ((2, third), (3, fourth), (1, pair), (0, slot)):
+            multiply(block_slot, unit, order)
             if len(held) > 1:
                 finish()
     while held:
@@ -469,17 +493,31 @@
                 if order == 0:
                     copy.wait_send()
 
+        @pl.when(inner == 0)
+        def _():
+            second_queries.wait_send()
+
         @pl.when(inner == 1)
         def _():
             for copy in query_forwards:
                 copy.wait_send()
 
 
-def add_kernel(pieces, out_ref):
-    result = pieces[0].astype(jnp.float32)
-    for part in range(1, pieces.shape[0]):
-        result = result + pieces[part].astype(jnp.float32)
-    out_ref[...] = result.astype(out_ref.dtype)
+def add_kernel(pieces, out_hbm, result, sems):
+    bands = sems.shape[0]
+    rows = result.shape[0] // bands
+    copies = []
+    for band in range(bands):
+        where = slice(band * rows, (band + 1) * rows)
+        total = pieces[0, where].astype(jnp.float32)
+        for part in range(1, pieces.shape[0]):
+            total = total + pieces[part, where].astype(jnp.float32)
+        result[where] = total.astype(result.dtype)
+        copy = pltpu.make_async_copy(result.at[where], out_hbm.at[where], sems.at[band])
+        copy.start()
+        copies.append(copy)
+    for copy in copies:
+        copy.wait()
 
 
 def local(queries, keys, values, segment_ids, out_weight):
@@ -502,50 +540,53 @@
     vmem = pl.BlockSpec(memory_space=pltpu.VMEM)
     bf16, f32 = jnp.bfloat16, jnp.float32
     dma = pltpu.SemaphoreType.DMA
+    buffers = [
+        pltpu.VMEM((1, HEAD_DIM), f32),
+        pltpu.VMEM(queries.shape, bf16),
+        pltpu.VMEM(keys.shape, bf16),
+        pltpu.VMEM((members, 1, rows), jnp.int32),
+        pltpu.VMEM((tiles, 2 * rows, HEAD_DIM), bf16),
+        pltpu.VMEM((tiles, 2 * rows, HEAD_DIM), bf16),
+        pltpu.VMEM((slots, rows, queries.shape[1]), bf16),
+        pltpu.VMEM((out_weight.shape[0], out_width), bf16),
+        pltpu.VMEM((slots, rows, queries.shape[1]), bf16),
+        pltpu.VMEM((group, rows, HEAD_DIM), f32),
+        pltpu.VMEM((group, rows, HEAD_DIM), f32),
+        pltpu.VMEM((group, rows, HEAD_DIM), f32),
+        pltpu.VMEM((tiles, group, rows, 2 * rows), f32),
+        pltpu.VMEM((slots * units, rows, half), bf16),
+        pltpu.VMEM((slots * units, rows, half), bf16),
+        pltpu.VMEM((2, rows, half), f32),
+        pltpu.VMEM((slots * units, rows, half), bf16),
+    ]
+    semaphores = [dma((5,))]
+    semaphores += [dma((members - 1,))] * 2
+    semaphores += [dma((slots - 1,))] * 4
+    semaphores += [dma((slots * (per - 1),))] * 4
+    semaphores += [dma((slots,))] * 2
+    semaphores += [dma((chunk_count * (per - 1),))] * 2
+    semaphores += [dma(()), pltpu.SemaphoreType.REGULAR]
+    semaphores += [dma((slots * units,))] * 3
+    semaphores += [dma((slots, units))]
+    on_chip = sum(math.prod(item.shape) * jnp.dtype(item.dtype).itemsize for item in buffers)
+    operands = (inverse, queries, keys, values, segment_ids.reshape(1, rows), out_weight)
     pieces = pl.pallas_call(
         functools.partial(layer_kernel, members, slots),
         out_shape=jax.ShapeDtypeStruct((slots // 2, rows, out_width), bf16),
         in_specs=[pl.BlockSpec(memory_space=pl.ANY)] * 6,
         out_specs=vmem,
-        scratch_shapes=[
-            pltpu.VMEM((1, HEAD_DIM), f32),
-            pltpu.VMEM(queries.shape, bf16),
-            pltpu.VMEM(keys.shape, bf16),
-            pltpu.VMEM((members, 1, rows), jnp.int32),
-            pltpu.VMEM((tiles, 2 * rows, HEAD_DIM), bf16),
-            pltpu.VMEM((tiles, 2 * rows, HEAD_DIM), bf16),
-            pltpu.VMEM((slots, rows, queries.shape[1]), bf16),
-            pltpu.VMEM((out_weight.shape[0], out_width), bf16),
-            pltpu.VMEM((slots, rows, queries.shape[1]), bf16),
-            pltpu.VMEM((group, rows, HEAD_DIM), f32),
-            pltpu.VMEM((group, rows, HEAD_DIM), f32),
-            pltpu.VMEM((group, rows, HEAD_DIM), f32),
-            pltpu.VMEM((tiles, group, rows, 2 * rows), f32),
-            pltpu.VMEM((slots * units, rows, half), bf16),
-            pltpu.VMEM((slots * units, rows, half), bf16),
-            pltpu.VMEM((2, rows, half), f32),
-            pltpu.VMEM((slots * units, rows, half), bf16),
-            dma((5,)),
-        ]
-        + [dma((members - 1,))] * 2
-        + [dma((slots - 1,))] * 4
-        + [dma((slots * (per - 1),))] * 4
-        + [dma((slots,))] * 2
-        + [dma((chunk_count * (per - 1),))] * 2
-        + [dma(())]
-        + [dma((slots * units,))] * 3
-        + [dma((slots, units))],
+        scratch_shapes=buffers + semaphores,
         compiler_params=pltpu.CompilerParams(
-            collective_id=0, has_side_effects=True, vmem_limit_bytes=60 * 1024 * 1024
+            collective_id=0, has_side_effects=True, vmem_limit_bytes=on_chip + 8 * 1024 * 1024
         ),
-    )(inverse, queries, keys, values, segment_ids.reshape(1, rows), out_weight)
-    band = rows // 4
+    )(*[pltpu.with_memory_space_constraint(x, pltpu.HBM) for x in operands])
     return pl.pallas_call(
         add_kernel,
-        grid=(rows // band,),
         out_shape=jax.ShapeDtypeStruct((rows, out_width), bf16),
-        in_specs=[pl.BlockSpec((slots // 2, band, out_width), lambda i: (0, i, 0))],
-        out_specs=pl.BlockSpec((band, out_width), lambda i: (i, 0)),
+        in_specs=[vmem],
+        out_specs=pl.BlockSpec(memory_space=pl.ANY),
+        scratch_shapes=[pltpu.VMEM((rows, out_width), bf16), dma((4,))],
+        compiler_params=pltpu.CompilerParams(vmem_limit_bytes=4 * 1024 * 1024),
     )(pieces)
 
 

time: 84.6 us -> 75.3 us (0.89); the launches traced: 83.2 us -> 75.1 us
  Pallas kernels: 83.2 us -> 75 us
    pallas_call x1, Pallas kernels: 79.7 us -> 74 us  [local(): pl.pallas_call(functools.partial(layer_kernel, members, slots), out_shape...]
    pallas_call x1, Pallas kernels: 3.48 us -> 0.95 us  [local(): pl.pallas_call(add_kernel, out_shape=jax.ShapeDtypeStruct((rows, out_widt...]
where the time goes in v2:
time: 75.3 us; the launch traced here: 75.1 us
  Pallas kernels  75 us (100%)
    pallas_call x1, Pallas kernels, local(): pl.pallas_call(functools.partial(layer_kernel, members, slots), out_shape...  74 us

profile of v2, /device:TPU:4, one launch (start us, length us, event | category | flops | bytes accessed | tf_op | source)
XLA Modules:
  0.0 75.1 jit_solution(11102611209126338532)
XLA Ops:
  0.0 74.0 %shard_map.64.pieces = bf16[2,192,2048]{2,1,0:T(8,128)(2,1)S(1)} custom-call(f32[1,128]{1,0:T(1,128)} %constant.2.clone.inverse_hbm, bf16[192,1024]{1,0:T(8,128)(2,1)} %q_hbm.1, bf16[192,128]{1,0:T(8,128)(2,1)} %k_hbm.1, bf16[192,128]{1,0:T(8,128)(2,1)} %v_hbm.1, s32[1,192]{1,0:T(1,128)} %bitcast.1, bf16[1024,1024]{1,0:T(8,128)(2,1)} %w_hbm.1), custom_call_target="tpu_custom_call" | custom-call | tf_op jit(solution)/shard_map/pallas_call | solution.py:573
  74.0 1.0 %shard_map.65 = bf16[192,2048]{1,0:T(8,128)(2,1)} custom-call(bf16[2,192,2048]{2,1,0:T(8,128)(2,1)S(1)} %shard_map.64.pieces), custom_call_target="tpu_custom_call" | custom-call | tf_op jit(solution)/shard_map/pallas_call | solution.py:583

commit v3 on v2

--- a/solution.py
+++ b/solution.py
@@ -34,9 +34,9 @@
 
 
 def layer_kernel(
-    members, slots, inverse_hbm, q_hbm, k_hbm, v_hbm, seg_hbm, w_hbm, recv,
+    members, slots, cuts, own_cuts, chunk_count, inverse_hbm, q_hbm, k_hbm, v_hbm, seg_hbm, w_hbm, recv,
     inverse_ref, q_ref, k_ref, seg_all, k_all, v_all, q_all, w_all, attended,
-    top, total, acc, scores_ref, half_send, half_recv, half_own, piece, in_sems,
+    top, total, acc, scores_ref, starts_ref, half_send, half_recv, half_own, piece, in_sems,
     seg_ss, seg_rs, k_ss, k_rs, v_ss, v_rs, k2_ss, k2_rs, v2_ss, v2_rs, q_ss, q_rs,
     w_ss, w_rs, own_sem, clear, d_ss, d_rs, c_ss, c_rs,
 ):
@@ -52,7 +52,7 @@
     place = lax.rem(me, per)
     core = lax.rem(g, 2)
     sibling = g + 1 - 2 * core
-    chunk_count = w_ss.shape[0] // (per - 1)
+    assert slots == 4 and q_ref.shape[1] == out_width // 2
 
     def part_of(ref, block):
         return ref.at[
@@ -139,51 +139,50 @@
     started = []
     seg_copies = start_all(
         [
-            send(seg_all.at[me], seg_all.at[me], seg_ss.at[d - 1], seg_rs.at[d - 1], lax.rem(me + d, members))
+            send(seg_all.at[me], seg_all.at[me], seg_ss, seg_rs, lax.rem(me + d, members))
             for d in range(1, members)
         ]
     )
-    started += seg_copies
+
+    def all_of(ref, send_sem, recv_sem):
+        return send(ref, ref, send_sem, recv_sem, me)
+
+    all_segs = all_of(seg_all.at[pl.ds(0, members - 1)], seg_ss, seg_rs)
     v_own = part_of(v_all, me)
     v_copies = start_all(to_slots(v_own, v_own, v_ss, v_rs))
     started += v_copies
     v_relays = start_all(relay(v_all, 0, v2_ss, v2_rs))
 
-    units = c_rs.shape[1]
-    if units > 1:
-        unit_width = out_width // units
-        own_units = units // per
-        unit_starts = [
-            lax.rem(place + u // own_units, per) * width + (u % own_units) * unit_width
-            for u in range(units)
-        ]
+    units = []
+    if len(cuts) > 1:
+        for r in range(per):
+            for first, size in cuts if r else own_cuts:
+                units.append((lax.rem(place + r, per) * width + first, size, r))
     else:
-        unit_width, own_units, unit_starts = width, 1, [0]
-    half = piece.shape[2]
-    column_chunks = width // unit_width
-    bands = chunk_count // column_chunks
-    band_rows = w_hbm.shape[0] // bands
-    w_copies = []
-    for c in range(chunk_count):
-        band = pl.ds((c % bands) * band_rows, band_rows)
-        first = (c // bands) * unit_width
-        target_columns = pl.ds(pl.multiple_of(place * width + first, unit_width), unit_width)
-        for r in range(1, per):
-            w_copies.append(
-                send(
-                    w_hbm.at[band, first : first + unit_width],
+        units.append((0, out_width, None))
+    w_copies, w_arrivals = [], {}
+    for cut, (first, size) in enumerate(cuts):
+        bands = chunk_count * size // width
+        band_rows = w_hbm.shape[0] // bands
+        for c in range(bands):
+            band = pl.ds(c * band_rows, band_rows)
+            target_columns = pl.ds(pl.multiple_of(place * width + first, size), size)
+            for r in range(1, per):
+                copy = send(
+                    w_hbm.at[band, first : first + size],
                     w_all.at[band, target_columns],
-                    w_ss.at[c * (per - 1) + r - 1],
-                    w_rs.at[c * (per - 1) + r - 1],
+                    w_ss.at[r - 1],
+                    w_rs.at[cut, r - 1],
                     slot * per + lax.rem(place + r, per),
                 )
-            )
+                w_copies.append(copy)
+        for r in range(1, per):
+            w_arrivals[per - r, first] = all_of(w_all.at[:, :size], w_ss.at[0], w_rs.at[cut, r - 1])
     early = per - 1
     start_all(w_copies[:early])
 
     with jax.named_scope("seg_wait"):
-        for copy in seg_copies:
-            copy.wait_recv()
+        all_segs.wait_recv()
 
     row_index = lax.broadcasted_iota(jnp.int32, (rows, 1), 0)
     position = (me * rows + row_index).astype(jnp.float32) - doc_start_column(
@@ -229,6 +228,11 @@
     def _():
         second_queries.start()
 
+
+    for other in range(slots):
+        starts_ref[other] = jnp.broadcast_to(
+            doc_start_column(seg_all, other * per + place, members, rows), (rows, HEAD_DIM)
+        ).astype(jnp.int32)
 
     for d in range(1, slots):
         with jax.named_scope(f"v_wait{d}"):
@@ -252,7 +256,7 @@
 
     def attend(block_slot):
         block = block_slot * per + place
-        start = doc_start_column(seg_all, block, members, rows).astype(jnp.int32)
+        start = starts_ref[block_slot]
         query_index = block * rows + lax.broadcasted_iota(jnp.int32, (rows, tile_rows), 0)
         first = lax.div(jnp.maximum(block - reach, 0), 2)
         last = lax.div(block, 2) + 1
@@ -266,7 +270,9 @@
                 key_index = number * tile_rows + lax.broadcasted_iota(
                     jnp.int32, (rows, tile_rows), 1
                 )
-                visible = (key_index <= query_index) & (key_index >= start)
+                visible = (key_index <= query_index) & (
+                    key_index >= jnp.concatenate([start] * len(parts), axis=1)
+                )
                 bias = jnp.where(visible, 0.0, masked_score)
                 key_tile = k_all[number]
                 for head in range(group):
@@ -314,52 +320,69 @@
                 ).astype(jnp.bfloat16)
 
     y_index = lax.div(g, 2)
-    step = min(256, half)
-    pair_copies, c_copies = [], []
-    held = []
-
-    def multiply(block_slot, unit, order):
-        index = order * units + unit
-        buffer = len(pair_copies) % half_own.shape[0]
-        kept = unit_starts[unit] + core * half
-        given = unit_starts[unit] + (1 - core) * half
-        for c in range(half // step):
-            half_send[index, :, c * step : (c + 1) * step] = jnp.dot(
-                attended[block_slot],
-                w_all[:, pl.ds(pl.multiple_of(given + c * step, step), step)],
-                preferred_element_type=jnp.float32,
-            ).astype(jnp.bfloat16)
-        across = pltpu.make_async_remote_copy(
-            src_ref=half_send.at[index],
-            dst_ref=half_recv.at[index],
-            send_sem=d_ss.at[index],
+
+    def across_copy(unit, block_slot, index, half):
+        where = unit if block_slot is None else (unit, block_slot)
+        where = (where, slice(None), slice(None), slice(half)) if block_slot is None else (
+            *where, slice(None), slice(half)
+        )
+        return pltpu.make_async_remote_copy(
+            src_ref=half_send.at[where],
+            dst_ref=half_recv.at[where],
+            send_sem=d_ss,
             recv_sem=d_rs.at[index],
             device_id={"tp": sibling},
             device_id_type=MESH,
         )
-        across.start()
-        pair_copies.append(across)
+
+    def multiply(block_slot, unit, given):
+        start, size, _ = units[unit]
+        half = size // 2
+        step = min(256, half)
+        first = start + (1 - core if given else core) * half
+        if block_slot is None:
+            left = attended[...].reshape(slots * rows, attended.shape[2])
+        else:
+            left = attended[block_slot]
         for c in range(half // step):
-            half_own[buffer, :, c * step : (c + 1) * step] = jnp.dot(
-                attended[block_slot],
-                w_all[:, pl.ds(pl.multiple_of(kept + c * step, step), step)],
+            lanes = slice(c * step, (c + 1) * step)
+            product = jnp.dot(
+                left,
+                w_all[:, pl.ds(pl.multiple_of(first + c * step, step), step)],
                 preferred_element_type=jnp.float32,
             )
-        held.append((block_slot, unit, order, index, buffer, kept, across))
-
-    def finish():
-        block_slot, unit, order, index, buffer, kept, across = held.pop(0)
-        with jax.named_scope(f"across_wait{index}"):
-            across.wait_recv()
-        piece[index] = (half_own[buffer] + half_recv[index].astype(jnp.float32)).astype(
-            jnp.bfloat16
-        )
+            if block_slot is None:
+                product = product.reshape(slots, rows, step)
+                where = (unit, slice(None), slice(None), lanes)
+            else:
+                where = (unit, block_slot, slice(None), lanes)
+            if given:
+                half_send[where] = product.astype(jnp.bfloat16)
+            else:
+                half_own[where[1:]] = product
+
+    def exchange(block_slot, unit, index):
+        copy = across_copy(unit, block_slot, index, units[unit][1] // 2)
+        copy.start()
+        return copy
+
+    def finish(block_slot, unit, order):
+        start, size, _ = units[unit]
+        half = size // 2
+        kept = start + core * half
+        lanes = slice(half)
+        index = order * len(units) + unit
+        piece[index, :, lanes] = (
+            half_own[block_slot, :, lanes]
+            + half_recv[unit, block_slot, :, lanes].astype(jnp.float32)
+        ).astype(jnp.bfloat16)
+        source = piece.at[index, :, lanes]
         target = recv.at[y_index, :, pl.ds(pl.multiple_of(kept, half), half)]
         copy = pltpu.make_async_remote_copy(
-            src_ref=piece.at[index],
+            src_ref=source,
             dst_ref=target,
-            send_sem=c_ss.at[index],
-            recv_sem=c_rs.at[g, unit],
+            send_sem=c_ss.at[min(order, 1)],
+            recv_sem=c_rs.at[g],
             device_id={"seq": block_slot * per + place, "tp": slot},
             device_id_type=MESH,
         )
@@ -367,14 +390,13 @@
 
             @pl.when(g == slot)
             def _():
-                target[...] = piece[index]
+                target[...] = source[...]
 
             @pl.when(g != slot)
             def _():
                 copy.start()
         else:
             copy.start()
-        c_copies.append((order, copy))
 
     def pass_on(block_slot, index):
         copy = send_queries(block_slot, pair, index)
@@ -388,14 +410,17 @@
         return copy
 
     def own_products(block_slot, order):
-        if units > 1:
+        if len(units) > 1:
             with jax.named_scope(f"product{order}"):
-                for unit in range(own_units):
-                    multiply(block_slot, unit, order)
-                    if len(held) > 1:
-                        finish()
-                while held:
-                    finish()
+                copies = []
+                for unit in range(len(own_cuts)):
+                    multiply(block_slot, unit, True)
+                    copies.append(exchange(block_slot, unit, unit * slots + order))
+                for unit in range(len(own_cuts)):
+                    multiply(block_slot, unit, False)
+                    with jax.named_scope(f"across_wait{unit}_{order}"):
+                        copies[unit].wait_recv()
+                    finish(block_slot, unit, order)
 
     second_block = pair + inner * (third - pair)
     third_block = third + inner * (fourth - third)
@@ -448,50 +473,42 @@
         attend(fourth_block)
     own_products(fourth_block, 3)
 
-    late = own_units if units > 1 else 0
-    for unit in range(late, units):
-        chunk = (unit % own_units) * bands
-        sender = unit // own_units - 1
+    for unit in range(len(own_cuts) if len(units) > 1 else 0, len(units)):
+        start, size, sender = units[unit]
         with jax.named_scope(f"w_wait{unit}"):
-            for c in range(chunk_count):
-                for r in range(per - 1):
-                    if units == 1 or (chunk <= c < chunk + bands and r == per - 2 - sender):
-                        w_copies[c * (per - 1) + r].wait_recv()
-        for order, block_slot in ((2, third), (3, fourth), (1, pair), (0, slot)):
-            multiply(block_slot, unit, order)
-            if len(held) > 1:
-                finish()
-    while held:
-        finish()
+            if sender is None:
+                for copy in w_arrivals.values():
+                    copy.wait_recv()
+            else:
+                w_arrivals[sender, cuts[(unit - len(own_cuts)) % len(cuts)][0]].wait_recv()
+        multiply(None, unit, True)
+        copy = exchange(None, unit, len(own_cuts) * slots + unit)
+        multiply(None, unit, False)
+        with jax.named_scope(f"across_wait{unit}"):
+            copy.wait_recv()
+        for order, block_slot in ((3, fourth), (2, third), (1, pair), (0, slot)):
+            finish(block_slot, unit, order)
 
     for source in range(tp_count):
-        for unit in range(units):
-            arrival = pltpu.make_async_remote_copy(
-                src_ref=piece.at[0],
-                dst_ref=recv.at[source // 2, :, :half],
-                send_sem=c_ss.at[0],
-                recv_sem=c_rs.at[source, unit],
-                device_id={"seq": me, "tp": sibling},
-                device_id_type=MESH,
-            )
-
-            @pl.when(jnp.logical_or(g != source, g != slot))
-            def _():
-                with jax.named_scope(f"arrive{source}_{unit}"):
-                    arrival.wait_recv()
+        arrival = all_of(recv.at[source // 2, :, : out_width // 2], c_ss.at[0], c_rs.at[source])
+
+        @pl.when(jnp.logical_or(g != source, g != slot))
+        def _():
+            with jax.named_scope(f"arrive{source}"):
+                arrival.wait_recv()
 
     with jax.named_scope("send_waits"):
-        for copy in started + w_copies + pair_copies:
+        all_segs.wait_send()
+        for copy in started:
             copy.wait_send()
-        for order, copy in c_copies:
-            if order > 0:
-                copy.wait_send()
+        for r in range(1, per):
+            all_of(w_all.at[:, :width], w_ss.at[r - 1], w_rs.at[0, 0]).wait_send()
+        all_of(attended, d_ss, d_rs.at[0]).wait_send()
+        all_of(attended.at[pl.ds(0, slots - 1)], c_ss.at[1], c_rs.at[0]).wait_send()
 
         @pl.when(g != slot)
         def _():
-            for order, copy in c_copies:
-                if order == 0:
-                    copy.wait_send()
+            all_of(attended.at[0], c_ss.at[0], c_rs.at[0]).wait_send()
 
         @pl.when(inner == 0)
         def _():
@@ -527,8 +544,16 @@
     per = members // slots
     heads = queries.shape[1] // HEAD_DIM
     out_width = out_weight.shape[1] * per
-    units = out_width // 512 if out_weight.shape[1] % 512 == 0 else 1
-    half = out_width // units // 2
+    width = out_weight.shape[1]
+    if width % 1024 == 0:
+        own_cuts = [(0, width // 2), (width // 2, width // 2)]
+        cuts = [(0, width // 2), (width // 2, width // 4), (3 * width // 4, width // 4)]
+        units = len(own_cuts) + (per - 1) * len(cuts)
+        half = width // 4
+    else:
+        own_cuts = cuts = [(0, width)]
+        units = 1
+        half = out_width // 2
     chunk_count = 16
     tiles = members // 2
     group = heads
@@ -554,27 +579,28 @@
         pltpu.VMEM((group, rows, HEAD_DIM), f32),
         pltpu.VMEM((group, rows, HEAD_DIM), f32),
         pltpu.VMEM((tiles, group, rows, 2 * rows), f32),
-        pltpu.VMEM((slots * units, rows, half), bf16),
-        pltpu.VMEM((slots * units, rows, half), bf16),
-        pltpu.VMEM((2, rows, half), f32),
+        pltpu.VMEM((slots, rows, HEAD_DIM), jnp.int32),
+        pltpu.VMEM((units, slots, rows, half), bf16),
+        pltpu.VMEM((units, slots, rows, half), bf16),
+        pltpu.VMEM((slots, rows, half), f32),
         pltpu.VMEM((slots * units, rows, half), bf16),
     ]
     semaphores = [dma((5,))]
-    semaphores += [dma((members - 1,))] * 2
+    semaphores += [dma(())] * 2
     semaphores += [dma((slots - 1,))] * 4
     semaphores += [dma((slots * (per - 1),))] * 4
     semaphores += [dma((slots,))] * 2
-    semaphores += [dma((chunk_count * (per - 1),))] * 2
+    semaphores += [dma((per - 1,)), dma((len(cuts), per - 1))]
     semaphores += [dma(()), pltpu.SemaphoreType.REGULAR]
-    semaphores += [dma((slots * units,))] * 3
-    semaphores += [dma((slots, units))]
+    semaphores += [dma(()), dma((len(own_cuts) * slots + units,)), dma((2,))]
+    semaphores += [dma((slots,))]
     on_chip = sum(math.prod(item.shape) * jnp.dtype(item.dtype).itemsize for item in buffers)
     operands = (inverse, queries, keys, values, segment_ids.reshape(1, rows), out_weight)
     pieces = pl.pallas_call(
-        functools.partial(layer_kernel, members, slots),
-        out_shape=jax.ShapeDtypeStruct((slots // 2, rows, out_width), bf16),
+        functools.partial(layer_kernel, members, slots, cuts, own_cuts, chunk_count),
+        out_shape=pltpu.VMEM((slots // 2, rows, out_width), bf16),
         in_specs=[pl.BlockSpec(memory_space=pl.ANY)] * 6,
-        out_specs=vmem,
+        out_specs=pl.BlockSpec(memory_space=pltpu.VMEM),
         scratch_shapes=buffers + semaphores,
         compiler_params=pltpu.CompilerParams(
             collective_id=0, has_side_effects=True, vmem_limit_bytes=on_chip + 8 * 1024 * 1024

time: 75.3 us -> 73.4 us (0.975)
  the two profiles are of different devices: /device:TPU:4 before, /device:TPU:1 now
where the time goes in v3:
time: 73.4 us; the launch traced here: 73.2 us
  Pallas kernels  73 us (99%)
    pallas_call x1, Pallas kernels, local(): pl.pallas_call(functools.partial(layer_kernel, members, slots, cuts, own_...  72.1 us

profile of v3, /device:TPU:1, one launch (start us, length us, event | category | flops | bytes accessed | tf_op | source)
XLA Modules:
  0.0 73.2 jit_solution(17369734969887324344)
XLA Ops:
  0.0 72.1 %shard_map.64.pieces = bf16[2,192,2048]{2,1,0:T(8,128)(2,1)S(1)} custom-call(f32[1,128]{1,0:T(1,128)} %constant.2.clone.inverse_hbm, bf16[192,1024]{1,0:T(8,128)(2,1)} %q_hbm.1, bf16[192,128]{1,0:T(8,128)(2,1)} %k_hbm.1, bf16[192,128]{1,0:T(8,128)(2,1)} %v_hbm.1, s32[1,192]{1,0:T(1,128)} %bitcast.1, bf16[1024,1024]{1,0:T(8,128)(2,1)} %w_hbm.1), custom_call_target="tpu_custom_call" | custom-call | tf_op jit(solution)/shard_map/pallas_call | solution.py:599
  72.1 1.0 %shard_map.65 = bf16[192,2048]{1,0:T(8,128)(2,1)} custom-call(bf16[2,192,2048]{2,1,0:T(8,128)(2,1)S(1)} %shard_map.64.pieces), custom_call_target="tpu_custom_call" | custom-call | tf_op jit(solution)/shard_map/pallas_call | solution.py:609

commit v4 on v3

--- a/solution.py
+++ b/solution.py
@@ -34,7 +34,7 @@
 
 
 def layer_kernel(
-    members, slots, cuts, own_cuts, chunk_count, inverse_hbm, q_hbm, k_hbm, v_hbm, seg_hbm, w_hbm, recv,
+    members, slots, cuts, own_cuts, solo, chunk_count, inverse_hbm, q_hbm, k_hbm, v_hbm, seg_hbm, w_hbm, recv,
     inverse_ref, q_ref, k_ref, seg_all, k_all, v_all, q_all, w_all, attended,
     top, total, acc, scores_ref, starts_ref, half_send, half_recv, half_own, piece, in_sems,
     seg_ss, seg_rs, k_ss, k_rs, v_ss, v_rs, k2_ss, k2_rs, v2_ss, v2_rs, q_ss, q_rs,
@@ -118,18 +118,26 @@
             for d in range(1, slots)
         ]
 
-    def relay(ref, d, ss, rs):
-        block = from_slot(d)
+    def relay(ref, block, index, ss, rs):
         return [
             send(
                 part_of(ref, block),
                 part_of(ref, block),
-                ss.at[d * (per - 1) + r - 1],
-                rs.at[d * (per - 1) + r - 1],
+                ss.at[index * (per - 1) + r - 1],
+                rs.at[index * (per - 1) + r - 1],
                 slot * per + lax.rem(place + r, per),
             )
             for r in range(1, per)
         ]
+
+    pair = slot + 1 - 2 * lax.rem(slot, 2)
+    inner = lax.rem(lax.div(slot + 1, 2), 2)
+    third = 2 - lax.div(slot, 2)
+    fourth = (slots - 1) * (1 - lax.div(slot, 2))
+
+    def send_keys(source, target_slot, send_sem):
+        block = part_of(k_all, source * per + place)
+        return send(block, block, send_sem, k_rs.at[source], target_slot * per + place)
 
     def start_all(copies):
         for copy in copies:
@@ -151,15 +159,24 @@
     v_own = part_of(v_all, me)
     v_copies = start_all(to_slots(v_own, v_own, v_ss, v_rs))
     started += v_copies
-    v_relays = start_all(relay(v_all, 0, v2_ss, v2_rs))
+    v_relays = start_all(relay(v_all, me, 0, v2_ss, v2_rs))
 
     units = []
     if len(cuts) > 1:
         for r in range(per):
             for first, size in cuts if r else own_cuts:
-                units.append((lax.rem(place + r, per) * width + first, size, r))
+                start = lax.rem(place + r, per) * width + first
+                units.append((start, size, r, None))
+        for u in range(len(units) - solo, len(units)):
+            units[u] = (*units[u][:3], u % 2)
     else:
-        units.append((0, out_width, None))
+        units.append((0, out_width, None, None))
+
+    def kept_part(unit):
+        start, size, _, keeper = units[unit]
+        if keeper is not None:
+            return start, start, size
+        return start + core * (size // 2), start + (1 - core) * (size // 2), size // 2
     w_copies, w_arrivals = [], {}
     for cut, (first, size) in enumerate(cuts):
         bands = chunk_count * size // width
@@ -199,18 +216,14 @@
 
     k_own = part_of(k_all, me)
     k_own[...] = rotated(k_ref[...])
-    k_copies = start_all(to_slots(k_own, k_own, k_ss, k_rs))
-    started += k_copies
-    k_relays = start_all(relay(k_all, 0, k2_ss, k2_rs))
+    started += start_all(
+        [send_keys(slot, to, k_ss.at[i]) for i, to in enumerate((pair, third, fourth))]
+    )
+    k_relays = start_all(relay(k_all, me, 0, k2_ss, k2_rs))
 
     for head in range(heads):
         lanes = slice(head * HEAD_DIM, (head + 1) * HEAD_DIM)
         q_all[slot, :, lanes] = rotated(q_ref[:, lanes])
-    pair = slot + 1 - 2 * lax.rem(slot, 2)
-    inner = lax.rem(lax.div(slot + 1, 2), 2)
-    third = 2 - lax.div(slot, 2)
-    fourth = (slots - 1) * (1 - lax.div(slot, 2))
-
     def send_queries(block_slot, target_slot, index):
         return send(
             q_all.at[block_slot],
@@ -221,13 +234,11 @@
         )
 
     first_queries, second_queries = send_queries(slot, pair, 0), send_queries(slot, third, 1)
-    first_queries.start()
-    started.append(first_queries)
+    started += start_all([first_queries])
 
     @pl.when(inner == 1)
     def _():
         second_queries.start()
-
 
     for other in range(slots):
         starts_ref[other] = jnp.broadcast_to(
@@ -237,11 +248,12 @@
     for d in range(1, slots):
         with jax.named_scope(f"v_wait{d}"):
             v_copies[d - 1].wait_recv()
-        v_relays += start_all(relay(v_all, d, v2_ss, v2_rs))
-    for d in range(1, slots):
-        with jax.named_scope(f"k_wait{d}"):
-            k_copies[d - 1].wait_recv()
-        k_relays += start_all(relay(k_all, d, k2_ss, k2_rs))
+        v_relays += start_all(relay(v_all, from_slot(d), d, v2_ss, v2_rs))
+    for i, source in enumerate((pair, third, fourth)):
+        with jax.named_scope(f"k_wait{i}"):
+            send_keys(source, pair, k_ss.at[0]).wait_recv()
+        k_relays += start_all(relay(k_all, source * per + place, i + 1, k2_ss, k2_rs))
+
     started += v_relays + k_relays
     start_all(w_copies[early:])
     with jax.named_scope("kv_relay_wait"):
@@ -254,7 +266,7 @@
 
     group = scores_ref.shape[1]
 
-    def attend(block_slot):
+    def attend(block_slot, between=None):
         block = block_slot * per + place
         start = starts_ref[block_slot]
         query_index = block * rows + lax.broadcasted_iota(jnp.int32, (rows, tile_rows), 0)
@@ -292,6 +304,8 @@
                 return unused
 
             lax.fori_loop(first, last, score_tile, 0)
+            if between is not None and base == 0:
+                between()
             for head in range(group):
                 top[head] = jnp.broadcast_to(
                     jnp.max(top[head], axis=1, keepdims=True), (rows, HEAD_DIM)
@@ -336,10 +350,9 @@
         )
 
     def multiply(block_slot, unit, given):
-        start, size, _ = units[unit]
-        half = size // 2
+        first, other, half = kept_part(unit)
+        first = other if given else first
         step = min(256, half)
-        first = start + (1 - core if given else core) * half
         if block_slot is None:
             left = attended[...].reshape(slots * rows, attended.shape[2])
         else:
@@ -362,14 +375,12 @@
                 half_own[where[1:]] = product
 
     def exchange(block_slot, unit, index):
-        copy = across_copy(unit, block_slot, index, units[unit][1] // 2)
+        copy = across_copy(unit, block_slot, index, kept_part(unit)[2])
         copy.start()
         return copy
 
     def finish(block_slot, unit, order):
-        start, size, _ = units[unit]
-        half = size // 2
-        kept = start + core * half
+        kept, _, half = kept_part(unit)
         lanes = slice(half)
         index = order * len(units) + unit
         piece[index, :, lanes] = (
@@ -439,23 +450,23 @@
             with jax.named_scope("q_wait_last"):
                 arrived.wait_recv()
 
+    def release_queries():
+        @pl.when(inner == 1)
+        def _():
+            with jax.named_scope("second_q_sent"):
+                second_queries.wait_send()
+            pl.semaphore_signal(
+                clear, inc=1, device_id={"seq": pair * per + place}, device_id_type=MESH
+            )
+
+        @pl.when(inner == 0)
+        def _():
+            with jax.named_scope("clear_wait"):
+                pl.semaphore_wait(clear, 1)
+            second_queries.start()
+
     with jax.named_scope("attend0"):
-        attend(slot)
-
-    @pl.when(inner == 1)
-    def _():
-        with jax.named_scope("second_q_sent"):
-            second_queries.wait_send()
-        pl.semaphore_signal(
-            clear, inc=1, device_id={"seq": pair * per + place}, device_id_type=MESH
-        )
-
-    @pl.when(inner == 0)
-    def _():
-        with jax.named_scope("clear_wait"):
-            pl.semaphore_wait(clear, 1)
-        second_queries.start()
-
+        attend(slot, release_queries)
     query_forwards.append(pass_on(third, 2))
     wait_queries(pair, only_outer=True)
     with jax.named_scope("attend1"):
@@ -474,20 +485,32 @@
     own_products(fourth_block, 3)
 
     for unit in range(len(own_cuts) if len(units) > 1 else 0, len(units)):
-        start, size, sender = units[unit]
+        _, _, sender, keeper = units[unit]
         with jax.named_scope(f"w_wait{unit}"):
             if sender is None:
                 for copy in w_arrivals.values():
                     copy.wait_recv()
             else:
                 w_arrivals[sender, cuts[(unit - len(own_cuts)) % len(cuts)][0]].wait_recv()
-        multiply(None, unit, True)
-        copy = exchange(None, unit, len(own_cuts) * slots + unit)
-        multiply(None, unit, False)
-        with jax.named_scope(f"across_wait{unit}"):
-            copy.wait_recv()
-        for order, block_slot in ((3, fourth), (2, third), (1, pair), (0, slot)):
-            finish(block_slot, unit, order)
+        index = len(own_cuts) * slots + unit
+
+        def give():
+            multiply(None, unit, True)
+            exchange(None, unit, index)
+
+        def keep():
+            multiply(None, unit, False)
+            with jax.named_scope(f"across_wait{unit}"):
+                across_copy(unit, None, index, kept_part(unit)[2]).wait_recv()
+            for order, block_slot in ((3, fourth), (2, third), (1, pair), (0, slot)):
+                finish(block_slot, unit, order)
+
+        if keeper is None:
+            give()
+            keep()
+        else:
+            pl.when(core == keeper)(keep)
+            pl.when(core != keeper)(give)
 
     for source in range(tp_count):
         arrival = all_of(recv.at[source // 2, :, : out_width // 2], c_ss.at[0], c_rs.at[source])
@@ -547,11 +570,14 @@
     width = out_weight.shape[1]
     if width % 1024 == 0:
         own_cuts = [(0, width // 2), (width // 2, width // 2)]
-        cuts = [(0, width // 2), (width // 2, width // 4), (3 * width // 4, width // 4)]
+        cuts = [(0, width // 2), (width // 2, width // 4)]
+        cuts += [(3 * width // 4, width // 8), (7 * width // 8, width // 8)]
+        solo = 2 if per == 2 else 0
         units = len(own_cuts) + (per - 1) * len(cuts)
         half = width // 4
     else:
         own_cuts = cuts = [(0, width)]
+        solo = 0
         units = 1
         half = out_width // 2
     chunk_count = 16
@@ -587,7 +613,7 @@
     ]
     semaphores = [dma((5,))]
     semaphores += [dma(())] * 2
-    semaphores += [dma((slots - 1,))] * 4
+    semaphores += [dma((slots - 1,)), dma((slots,))] + [dma((slots - 1,))] * 2
     semaphores += [dma((slots * (per - 1),))] * 4
     semaphores += [dma((slots,))] * 2
     semaphores += [dma((per - 1,)), dma((len(cuts), per - 1))]
@@ -597,7 +623,7 @@
     on_chip = sum(math.prod(item.shape) * jnp.dtype(item.dtype).itemsize for item in buffers)
     operands = (inverse, queries, keys, values, segment_ids.reshape(1, rows), out_weight)
     pieces = pl.pallas_call(
-        functools.partial(layer_kernel, members, slots, cuts, own_cuts, chunk_count),
+        functools.partial(layer_kernel, members, slots, cuts, own_cuts, solo, chunk_count),
         out_shape=pltpu.VMEM((slots // 2, rows, out_width), bf16),
         in_specs=[pl.BlockSpec(memory_space=pl.ANY)] * 6,
         out_specs=pl.BlockSpec(memory_space=pltpu.VMEM),

time: 73.4 us -> 72 us (0.981)
  the two profiles are of different devices: /device:TPU:1 before, /device:TPU:4 now
where the time goes in v4:
time: 72 us; the launch traced here: 71.9 us
  Pallas kernels  71.7 us (100%)
    pallas_call x1, Pallas kernels, local(): pl.pallas_call(functools.partial(layer_kernel, members, slots, cuts, own_...  70.8 us

profile of v4, /device:TPU:4, one launch (start us, length us, event | category | flops | bytes accessed | tf_op | source)
XLA Modules:
  0.0 71.9 jit_solution(12629257928917624278)
XLA Ops:
  0.0 70.8 %shard_map.64.pieces = bf16[2,192,2048]{2,1,0:T(8,128)(2,1)S(1)} custom-call(f32[1,128]{1,0:T(1,128)} %constant.2.clone.inverse_hbm, bf16[192,1024]{1,0:T(8,128)(2,1)} %q_hbm.1, bf16[192,128]{1,0:T(8,128)(2,1)} %k_hbm.1, bf16[192,128]{1,0:T(8,128)(2,1)} %v_hbm.1, s32[1,192]{1,0:T(1,128)} %bitcast.1, bf16[1024,1024]{1,0:T(8,128)(2,1)} %w_hbm.1), custom_call_target="tpu_custom_call" | custom-call | tf_op jit(solution)/shard_map/pallas_call | solution.py:625
  70.8 1.0 %shard_map.65 = bf16[192,2048]{1,0:T(8,128)(2,1)} custom-call(bf16[2,192,2048]{2,1,0:T(8,128)(2,1)S(1)} %shard_map.64.pieces), custom_call_target="tpu_custom_call" | custom-call | tf_op jit(solution)/shard_map/pallas_call | solution.py:635

commit v5 on v4

--- a/solution.py
+++ b/solution.py
@@ -37,7 +37,7 @@
     members, slots, cuts, own_cuts, solo, chunk_count, inverse_hbm, q_hbm, k_hbm, v_hbm, seg_hbm, w_hbm, recv,
     inverse_ref, q_ref, k_ref, seg_all, k_all, v_all, q_all, w_all, attended,
     top, total, acc, scores_ref, starts_ref, half_send, half_recv, half_own, piece, in_sems,
-    seg_ss, seg_rs, k_ss, k_rs, v_ss, v_rs, k2_ss, k2_rs, v2_ss, v2_rs, q_ss, q_rs,
+    seg_ss, seg_rs, kv_ss, k_rs, v_rs, x_ss, x_rs, q_ss, q_rs,
     w_ss, w_rs, own_sem, clear, d_ss, d_rs, c_ss, c_rs,
 ):
     rows = q_ref.shape[0]
@@ -52,7 +52,7 @@
     place = lax.rem(me, per)
     core = lax.rem(g, 2)
     sibling = g + 1 - 2 * core
-    assert slots == 4 and q_ref.shape[1] == out_width // 2
+    assert slots == 4 and q_ref.shape[1] == out_width // 2 == 2 * slots * HEAD_DIM
 
     def part_of(ref, block):
         return ref.at[
@@ -114,17 +114,17 @@
 
     def to_slots(source, target, ss, rs):
         return [
-            send(source, target, ss.at[d - 1], rs.at[d - 1], lax.rem(slot + d, slots) * per + place)
+            send(source, target, ss, rs.at[d - 1], lax.rem(slot + d, slots) * per + place)
             for d in range(1, slots)
         ]
 
-    def relay(ref, block, index, ss, rs):
+    def relay(ref, block, ss, rs):
         return [
             send(
                 part_of(ref, block),
                 part_of(ref, block),
-                ss.at[index * (per - 1) + r - 1],
-                rs.at[index * (per - 1) + r - 1],
+                ss.at[r - 1],
+                rs.at[r - 1],
                 slot * per + lax.rem(place + r, per),
             )
             for r in range(1, per)
@@ -157,9 +157,8 @@
 
     all_segs = all_of(seg_all.at[pl.ds(0, members - 1)], seg_ss, seg_rs)
     v_own = part_of(v_all, me)
-    v_copies = start_all(to_slots(v_own, v_own, v_ss, v_rs))
-    started += v_copies
-    v_relays = start_all(relay(v_all, me, 0, v2_ss, v2_rs))
+    v_copies = start_all(to_slots(v_own, v_own, kv_ss, v_rs))
+    v_relays = start_all(relay(v_all, me, x_ss, x_rs))
 
     units = []
     if len(cuts) > 1:
@@ -216,10 +215,10 @@
 
     k_own = part_of(k_all, me)
     k_own[...] = rotated(k_ref[...])
-    started += start_all(
-        [send_keys(slot, to, k_ss.at[i]) for i, to in enumerate((pair, third, fourth))]
+    start_all(
+        [send_keys(slot, to, kv_ss) for to in (pair, third, fourth)]
     )
-    k_relays = start_all(relay(k_all, me, 0, k2_ss, k2_rs))
+    k_relays = start_all(relay(k_all, me, x_ss, x_rs))
 
     for head in range(heads):
         lanes = slice(head * HEAD_DIM, (head + 1) * HEAD_DIM)
@@ -248,17 +247,16 @@
     for d in range(1, slots):
         with jax.named_scope(f"v_wait{d}"):
             v_copies[d - 1].wait_recv()
-        v_relays += start_all(relay(v_all, from_slot(d), d, v2_ss, v2_rs))
+        v_relays += start_all(relay(v_all, from_slot(d), x_ss, x_rs))
     for i, source in enumerate((pair, third, fourth)):
         with jax.named_scope(f"k_wait{i}"):
-            send_keys(source, pair, k_ss.at[0]).wait_recv()
-        k_relays += start_all(relay(k_all, source * per + place, i + 1, k2_ss, k2_rs))
-
-    started += v_relays + k_relays
+            send_keys(source, pair, kv_ss).wait_recv()
+        k_relays += start_all(relay(k_all, source * per + place, x_ss, x_rs))
+
     start_all(w_copies[early:])
     with jax.named_scope("kv_relay_wait"):
-        for copy in v_relays + k_relays:
-            copy.wait_recv()
+        for r in range(1, per):
+            all_of(q_ref, x_ss.at[r - 1], x_rs.at[r - 1]).wait_recv()
 
     tile_rows = k_all.shape[1]
     reach = -(-(3 * members * rows // 4 - 1) // rows)
@@ -522,9 +520,11 @@
 
     with jax.named_scope("send_waits"):
         all_segs.wait_send()
+        all_of(q_ref.at[:, : 2 * (slots - 1) * HEAD_DIM], kv_ss, x_rs.at[0]).wait_send()
         for copy in started:
             copy.wait_send()
         for r in range(1, per):
+            all_of(q_ref, x_ss.at[r - 1], x_rs.at[r - 1]).wait_send()
             all_of(w_all.at[:, :width], w_ss.at[r - 1], w_rs.at[0, 0]).wait_send()
         all_of(attended, d_ss, d_rs.at[0]).wait_send()
         all_of(attended.at[pl.ds(0, slots - 1)], c_ss.at[1], c_rs.at[0]).wait_send()
@@ -613,8 +613,8 @@
     ]
     semaphores = [dma((5,))]
     semaphores += [dma(())] * 2
-    semaphores += [dma((slots - 1,)), dma((slots,))] + [dma((slots - 1,))] * 2
-    semaphores += [dma((slots * (per - 1),))] * 4
+    semaphores += [dma(()), dma((slots,)), dma((slots - 1,))]
+    semaphores += [dma((per - 1,))] * 2
     semaphores += [dma((slots,))] * 2
     semaphores += [dma((per - 1,)), dma((len(cuts), per - 1))]
     semaphores += [dma(()), pltpu.SemaphoreType.REGULAR]

time: 72 us -> 71.8 us (level)
  no operation moved by 1% of the time
where the time goes in v5:
time: 71.8 us; the launch traced here: 71.7 us
  Pallas kernels  71.5 us (100%)
    pallas_call x1, Pallas kernels, local(): pl.pallas_call(functools.partial(layer_kernel, members, slots, cuts, own_...  70.6 us

profile of v5, /device:TPU:4, one launch (start us, length us, event | category | flops | bytes accessed | tf_op | source)
XLA Modules:
  0.0 71.7 jit_solution(13341630700257438750)
XLA Ops:
  0.0 70.6 %shard_map.64.pieces = bf16[2,192,2048]{2,1,0:T(8,128)(2,1)S(1)} custom-call(f32[1,128]{1,0:T(1,128)} %constant.2.clone.inverse_hbm, bf16[192,1024]{1,0:T(8,128)(2,1)} %q_hbm.1, bf16[192,128]{1,0:T(8,128)(2,1)} %k_hbm.1, bf16[192,128]{1,0:T(8,128)(2,1)} %v_hbm.1, s32[1,192]{1,0:T(1,128)} %bitcast.1, bf16[1024,1024]{1,0:T(8,128)(2,1)} %w_hbm.1), custom_call_target="tpu_custom_call" | custom-call | tf_op jit(solution)/shard_map/pallas_call | solution.py:625
  70.6 1.0 %shard_map.65 = bf16[192,2048]{1,0:T(8,128)(2,1)} custom-call(bf16[2,192,2048]{2,1,0:T(8,128)(2,1)S(1)} %shard_map.64.pieces), custom_call_target="tpu_custom_call" | custom-call | tf_op jit(solution)/shard_map/pallas_call | solution.py:635
